TPU v7x, 32 devices: a whole 2x2x4 slice. The times are simulated.
32 devices in a mesh: vocab: 8 (over z, x), group: 4 (over y, core).
Axes of the slice: x: 2, y: 2, z: 4, core: 2. Of those that a mesh axis runs over, the one named last changes fastest.
Arguments:
- hidden_states: bfloat16 [512, 4096], P(('group', 'vocab')), parts along dimension 0, may hold values from -32 to 32
- head_weight: bfloat16 [4096, 19456], P(None, 'vocab'), may hold values from -1 to 1
- pick_index: int32 [512, 64], P('group'), parts along dimension 0, may hold values from 0 to 19455, as said below
- owner_order: int32 [512], P('group'), parts along dimension 0, may hold values from 0 to 127, each once
Outputs:
- token_logprobs: float32 [512, 64], P(('group', 'vocab')), parts along dimension 0
- token_logtotal: float32 [512], P(('group', 'vocab')), parts along dimension 0
There are 4 independent parts, one for each index of `group`. A program takes and returns all parts, laid end to end along the dimension named above; an argument that names none is the same for every part. Nothing has to cross between parts.
Inputs may be any that keep to these rules, and one draw needn't show every extreme that they name: `pick_index`: each row holds 64 distinct vocabulary entries. `owner_order`: each token appears once.
All inputs are finite; a program needn't handle non-finite values.
Results may differ from a plain program's by a relative error of at most 0.0003.
Values may be sent and summed in bfloat16 or wider, within the bound.
A program may use at most 128 MiB of HBM per device.

v0:
```python
import math

import jax
import jax.numpy as jnp
from jax import lax
from jax.sharding import PartitionSpec as P


def select_block(pair):
    block_logits, block_index = pair
    columns = lax.broadcasted_iota(jnp.int32, (1, 1, block_logits.shape[1]), 2)
    matches = block_index[:, :, None] == columns
    return jnp.sum(jnp.where(matches, block_logits[:, None, :], 0.0), axis=2)


def local(hidden_states, head_weight, pick_index, owner_order):
    shard_count = lax.axis_size("vocab")
    shard_width = head_weight.shape[1]
    shard_index = lax.axis_index("vocab")
    shard_start = shard_index * shard_width
    own_rows = hidden_states.shape[0]
    pick_count = pick_index.shape[1]
    all_rows = pick_index.shape[0]
    logits = jnp.dot(
        lax.all_gather(hidden_states, "vocab", axis=0, tiled=True),
        head_weight,
        preferred_element_type=jnp.float32,
    )
    local_index = pick_index - shard_start
    block_size = math.gcd(all_rows, 32)
    block_count = all_rows // block_size
    picked = lax.map(
        select_block,
        (
            logits.reshape(block_count, block_size, shard_width),
            local_index.reshape(block_count, block_size, pick_count),
        ),
    )
    picked = picked.reshape(all_rows, pick_count)
    picked = jnp.take(picked, owner_order, axis=0)
    local_max = jnp.max(logits, axis=1)
    local_sum = jnp.sum(jnp.exp(logits - local_max[:, None]), axis=1)
    sent_max = jnp.take(local_max, owner_order, axis=0).reshape(shard_count, own_rows)
    sent_sum = jnp.take(local_sum, owner_order, axis=0).reshape(shard_count, own_rows)
    sent_picks = picked.reshape(shard_count, own_rows, pick_count)
    received_picks, maxima, totals = (
        lax.all_to_all(sent_picks, "vocab", split_axis=0, concat_axis=0, tiled=True),
        lax.all_to_all(sent_max, "vocab", split_axis=0, concat_axis=0, tiled=True),
        lax.all_to_all(sent_sum, "vocab", split_axis=0, concat_axis=0, tiled=True),
    )
    overall_max = jnp.max(maxima, axis=0)
    log_total = overall_max + jnp.log(
        jnp.sum(totals * jnp.exp(maxima - overall_max[None, :]), axis=0)
    )
    logprobs = jnp.sum(received_picks, axis=0) - log_total[:, None]
    return (logprobs, log_total)


def solution(mesh):
    in_specs = (P(("group", "vocab"), None), P(None, "vocab"), P("group", None), P("group"))
    out_specs = (P(("group", "vocab"), None), P(("group", "vocab")))
    return jax.shard_map(local, mesh=mesh, in_specs=in_specs, out_specs=out_specs, check_vma=False)
```

profile of v0, /device:TPU:0, one launch (start us, length us, event | category | flops | bytes accessed | tf_op | source)
XLA Modules:
  0.0 113.9 jit_solution(2473637600932250623)
XLA Ops:
  7.2 0.0 copy-start.1
  7.2 0.0 all-gather.2.cloned.1.call-start
  7.2 0.7 all-gather.2.cloned.1.call-update
  7.9 0.8 broadcast_subtract_fusion
  8.7 0.1 copy.11
  8.8 0.7 compare_select_fusion
  9.5 43.7 %all-gather.2.cloned.1.call-done = bf16[128,4096]{1,0:T(8,128)(2,1)} async-done(((bf16[16,4096]{1,0:T(8,128)(2,1)}), bf16[128,4096]{1,0:T(8,128)(2,1)}) %all-gather.2.cloned.1.call-update) | async-done | bytes 1048592 | tf_op jit(solution)/shard_map/all_gather | solution.py:25
  53.1 10.0 %fusion = (f32[128]{0:T(128)S(1)}, f32[128,2432]{1,0:T(8,128)S(1)}) fusion(bf16[128,4096]{1,0:T(8,128)(2,1)} %all-gather.2.cloned.1.call-done, bf16[4096,2432]{1,0:T(8,128)(2,1)} %param.9), kind=kOutput, calls=%fused_computation.19 | convolution fusion | flops 2550448128 | bytes 22217216 | tf_op jit(solution)/shard_map/dot_general | solution.py:24
  63.1 0.3 exponential_reduce_fusion
  63.5 1.2 %gather_fusion.1 = f32[128]{0:T(128)S(1)} fusion(f32[128]{0:T(128)S(1)} %get-tuple-element.36, s32[1024]{0:T(1024)S(1)} %pad_clamp_fusion), kind=kCustom, calls=%fused_computation.clone | custom fusion | bytes 1536 | tf_op jit(solution)/shard_map/jit(_take)/gather | solution.py:43
  64.7 1.2 %gather_fusion.2 = f32[128]{0:T(128)S(1)} fusion(f32[128]{0:T(128)S(1)} %exponential_reduce_fusion, s32[1024]{0:T(1024)S(1)} %pad_clamp_fusion), kind=kCustom, calls=%fused_computation.1.clone | custom fusion | bytes 1536 | tf_op jit(solution)/shard_map/jit(_take)/gather | solution.py:44
  65.9 0.0 copy-done.1
  66.0 0.7 all_to_all.20
  66.6 3.3 %all-to-all-start.1 = ((f32[8,1,16]{2,1,0:T(1,128)}), f32[8,1,16]{2,1,0:T(1,128)S(1)}, u32[]{:S(2)}, u32[]{:S(2)}) async-start(f32[8,1,16]{2,1,0:T(1,128)} %bitcast.7), calls=%async_computation.1 | async-start | bytes 8192 | tf_op jit(solution)/shard_map/all_to_all | solution.py:48
  70.0 11.3 %while.10 = (s32[]{:T(128)}, f32[4,32,64]{2,1,0:T(8,128)S(1)}, s32[4,32,64]{2,1,0:T(8,128)S(1)}, f32[4,32,2432]{2,1,0:T(8,128)S(1)}, s32[]{:T(128)}) while((s32[]{:T(128)}, f32[4,32,64]{2,1,0:T(8,128)S(1)}, s32[4,32,64]{2,1,0:T(8,128)S(1)}, f32[4,32,2432]{2,1,0:T(8,128)S(1)}, s32[]{:T(128)}) %tuple.31), condition=%wide.region_2.3_spmd, body=%wide.region_0.2_spmd.sunk | while | flops 14940162 | bytes 999497 | solution.py:32
  70.0 2.7 %select_reduce_fusion.2 = f32[32,64]{1,0:T(8,128)S(1)} fusion(f32[32,2432]{1,0:T(8,128)S(1)} %dynamic-slice_bitcast_fusion.4, s32[32,64]{1,0:T(8,128)S(1)} %dynamic-slice_bitcast_fusion.5), kind=kLoop, calls=%fused_computation.3.clone.1 | loop fusion | flops 14940160 | bytes 327680 | tf_op jit(solution)/shard_map/while/body/eval_jaxpr/reduce_sum | solution.py:13
  72.8 2.7 %select_reduce_fusion.2 = f32[32,64]{1,0:T(8,128)S(1)} fusion(f32[32,2432]{1,0:T(8,128)S(1)} %dynamic-slice_bitcast_fusion.4, s32[32,64]{1,0:T(8,128)S(1)} %dynamic-slice_bitcast_fusion.5), kind=kLoop, calls=%fused_computation.3.clone.1 | loop fusion | flops 14940160 | bytes 327680 | tf_op jit(solution)/shard_map/while/body/eval_jaxpr/reduce_sum | solution.py:13
  75.6 2.7 %select_reduce_fusion.2 = f32[32,64]{1,0:T(8,128)S(1)} fusion(f32[32,2432]{1,0:T(8,128)S(1)} %dynamic-slice_bitcast_fusion.4, s32[32,64]{1,0:T(8,128)S(1)} %dynamic-slice_bitcast_fusion.5), kind=kLoop, calls=%fused_computation.3.clone.1 | loop fusion | flops 14940160 | bytes 327680 | tf_op jit(solution)/shard_map/while/body/eval_jaxpr/reduce_sum | solution.py:13
  78.5 2.7 %select_reduce_fusion.2 = f32[32,64]{1,0:T(8,128)S(1)} fusion(f32[32,2432]{1,0:T(8,128)S(1)} %dynamic-slice_bitcast_fusion.4, s32[32,64]{1,0:T(8,128)S(1)} %dynamic-slice_bitcast_fusion.5), kind=kLoop, calls=%fused_computation.3.clone.1 | loop fusion | flops 14940160 | bytes 327680 | tf_op jit(solution)/shard_map/while/body/eval_jaxpr/reduce_sum | solution.py:13
  81.2 0.1 broadcast_in_dim.46
  81.3 0.7 all_to_all.22
  82.0 0.6 gather_fusion
  82.6 0.0 all-to-all-done.1
  82.6 6.0 %all-to-all-start.2 = ((f32[8,1,16]{2,1,0:T(1,128)}), f32[8,1,16]{2,1,0:T(1,128)S(1)}, u32[]{:S(2)}, u32[]{:S(2)}) async-start(f32[8,1,16]{2,1,0:T(1,128)} %bitcast.8), calls=%async_computation.2 | async-start | bytes 8192 | tf_op jit(solution)/shard_map/all_to_all | solution.py:49
  88.6 0.1 broadcast_select_fusion
  88.7 0.7 reshape.84
  89.4 5.7 %all-to-all-done.2 = f32[8,1,16]{2,1,0:T(1,128)S(1)} async-done(((f32[8,1,16]{2,1,0:T(1,128)}), f32[8,1,16]{2,1,0:T(1,128)S(1)}, u32[]{:S(2)}, u32[]{:S(2)}) %all-to-all-start.2) | async-done | bytes 544 | tf_op jit(solution)/shard_map/all_to_all | solution.py:49
  95.1 3.3 %all-to-all-start = ((f32[8,1,1024]{2,1,0:T(1,128)}), f32[8,1,1024]{2,1,0:T(1,128)S(1)}, u32[]{:S(2)}, u32[]{:S(2)}) async-start(f32[8,1,1024]{2,1,0:T(1,128)} %reshape.84), calls=%async_computation | async-start | bytes 65536 | tf_op jit(solution)/shard_map/all_to_all | solution.py:47
  98.5 0.0 copy-start
  98.5 6.6 %all-to-all-done = f32[8,1,1024]{2,1,0:T(1,128)S(1)} async-done(((f32[8,1,1024]{2,1,0:T(1,128)}), f32[8,1,1024]{2,1,0:T(1,128)S(1)}, u32[]{:S(2)}, u32[]{:S(2)}) %all-to-all-start) | async-done | bytes 32800 | tf_op jit(solution)/shard_map/all_to_all | solution.py:47
  105.1 0.5 broadcast.17
  105.6 0.7 reduce.1
  106.3 0.1 reshape.85
  106.4 0.7 broadcast_subtract_fusion.1
  107.1 0.0 copy-done
  (20 shorter events, 0.3 us)
Async XLA Ops:
  7.2 58.8 %copy-start.1 = (s32[128]{0:T(128)S(1)}, s32[128]{0:T(128)}, u32[]{:S(2)}) copy-start(s32[128]{0:T(128)} %param.11) | copy-start | bytes 1540
  7.2 46.0 %all-gather.2.cloned.1.call-start = ((), (), s32[]{:S(2)}) async-start(), calls=%async_computation.3 | async-start | bytes 1179648 | tf_op jit(solution)/shard_map/all_gather | solution.py:25
  66.6 16.0 %all-to-all-start.1 = ((f32[8,1,16]{2,1,0:T(1,128)}), f32[8,1,16]{2,1,0:T(1,128)S(1)}, u32[]{:S(2)}, u32[]{:S(2)}) async-start(f32[8,1,16]{2,1,0:T(1,128)} %bitcast.7), calls=%async_computation.1 | async-start | bytes 8192 | tf_op jit(solution)/shard_map/all_to_all | solution.py:48
  82.6 12.5 %all-to-all-start.2 = ((f32[8,1,16]{2,1,0:T(1,128)}), f32[8,1,16]{2,1,0:T(1,128)S(1)}, u32[]{:S(2)}, u32[]{:S(2)}) async-start(f32[8,1,16]{2,1,0:T(1,128)} %bitcast.8), calls=%async_computation.2 | async-start | bytes 8192 | tf_op jit(solution)/shard_map/all_to_all | solution.py:49
  95.1 10.0 %all-to-all-start = ((f32[8,1,1024]{2,1,0:T(1,128)}), f32[8,1,1024]{2,1,0:T(1,128)S(1)}, u32[]{:S(2)}, u32[]{:S(2)}) async-start(f32[8,1,1024]{2,1,0:T(1,128)} %reshape.84), calls=%async_computation | async-start | bytes 65536 | tf_op jit(solution)/shard_map/all_to_all | solution.py:47
  98.5 8.6 %copy-start = (f32[16]{0:T(128)}, f32[16]{0:T(128)S(1)}, u32[]{:S(2)}) copy-start(f32[16]{0:T(128)S(1)} %log_add_fusion) | copy-start | bytes 196
Sparse Core Ops, SparseCore 0:
  10.1 42.9 all-gather.1
where the time goes:
time: 114 us
  waiting for transfers between devices  56.6 us (50%)
  other arithmetic  14.3 us (13%)
  between operations  14.1 us (12%)
  starting transfers between devices  12.7 us (11%)
  matrix products  9.97 us (9%)
  local copies, waits for them, and re-layouts  6.11 us (5%)
    all_gather x1, waiting for transfers between devices, local(): lax.all_gather(hidden_states, 'vocab', axis=0, tiled=True)  43.7 us
    reduce_sum x4, other arithmetic, select_block(): return jnp.sum(jnp.where(matches, block_logits[:, None, :], 0.0), axis=2)  11 us
    dot_general x1, matrix products, local(): jnp.dot(lax.all_gather(hidden_states, 'vocab', axis=0, tiled=True), head_...  9.97 us
    all_to_all x1, waiting for transfers between devices, local(): lax.all_to_all(sent_picks, 'vocab', split_axis=0, concat_axis=0, tiled=True)  6.58 us
    all_to_all x1, starting transfers between devices, local(): lax.all_to_all(sent_sum, 'vocab', split_axis=0, concat_axis=0, tiled=True)  5.98 us
    all_to_all x1, waiting for transfers between devices, local(): lax.all_to_all(sent_sum, 'vocab', split_axis=0, concat_axis=0, tiled=True)  5.67 us
    all_to_all x1, starting transfers between devices, local(): lax.all_to_all(sent_picks, 'vocab', split_axis=0, concat_axis=0, tiled=True)  3.33 us
    all_to_all x1, starting transfers between devices, local(): lax.all_to_all(sent_max, 'vocab', split_axis=0, concat_axis=0, tiled=True)  3.32 us
  transfers between devices with their start and end apart: 4, of which 3 were waited for; matrix products, arithmetic and copies ran while one was open for 13% of the time, Pallas kernels for 0%

commit v1 on v0

v1 whole, which is shorter than its diff:
```python
import functools

import jax
import jax.numpy as jnp
from jax import lax
from jax.experimental import pallas as pl
from jax.experimental.pallas import tpu as pltpu
from jax.sharding import PartitionSpec as P

MESH = pl.DeviceIdType.MESH
LANES = 128


def kernel(
    n, chunks,
    hid, weight, pick, order,
    logprobs, logtotal,
    gathered, held, logits, stage, outbox, inbox,
    weight_sem, own_sem, far_send, far_recv, near_send, near_recv, end_send, end_recv,
):
    me = lax.axis_index("vocab")
    rows, depth = hid.shape
    tokens = gathered.shape[0]
    width = weight.shape[1]
    picks = pick.shape[1]
    kc = depth // chunks
    pair = 2 if n % 2 == 0 else 1
    outer = n // pair
    pos, side = me // pair, me % pair
    partner = me + 1 - 2 * side

    def columns(c):
        return pl.ds(c * kc, kc)

    def block(owner, c):
        return gathered.at[pl.ds(pl.multiple_of(owner * rows, rows), rows), columns(c)]

    weight_copies = []
    for c in range(chunks):
        copy = pltpu.make_async_copy(weight.at[columns(c), :], held.at[columns(c), :], weight_sem.at[c])
        copy.start()
        weight_copies.append(copy)
    own = pltpu.make_async_copy(hid, gathered.at[pl.ds(pl.multiple_of(me * rows, rows), rows), :], own_sem)
    own.start()

    barrier = pltpu.get_barrier_semaphore()
    for j in range(1, n):
        pl.semaphore_signal(barrier, inc=1, device_id={"vocab": lax.rem(me + j, n)}, device_id_type=MESH)
    pl.semaphore_wait(barrier, n - 1)

    far = [[] for _ in range(chunks)]
    near = [[] for _ in range(chunks)]
    for c in range(chunks):
        for j in range(1, outer):
            copy = pltpu.make_async_remote_copy(
                src_ref=hid.at[:, columns(c)], dst_ref=block(me, c),
                send_sem=far_send.at[c, j - 1], recv_sem=far_recv.at[c, j - 1],
                device_id={"vocab": lax.rem(pos + j, outer) * pair + side}, device_id_type=MESH,
            )
            copy.start()
            far[c].append(copy)
        if pair == 2:
            copy = pltpu.make_async_remote_copy(
                src_ref=hid.at[:, columns(c)], dst_ref=block(me, c),
                send_sem=near_send.at[c, 0], recv_sem=near_recv.at[c, 0],
                device_id={"vocab": partner}, device_id_type=MESH,
            )
            copy.start()
            near[c].append(copy)

    for step in range(chunks + 1):
        if step < chunks:
            c = step
            for j in range(1, outer):
                far[c][j - 1].wait_recv()
                if pair == 2:
                    source = lax.rem(pos - j + outer, outer) * pair + side
                    copy = pltpu.make_async_remote_copy(
                        src_ref=block(source, c), dst_ref=block(source, c),
                        send_sem=near_send.at[c, j], recv_sem=near_recv.at[c, j],
                        device_id={"vocab": partner}, device_id_type=MESH,
                    )
                    copy.start()
                    near[c].append(copy)
        if step >= 1:
            c = step - 1
            if c == 0:
                own.wait()
            for copy in near[c]:
                copy.wait_recv()
            weight_copies[c].wait()
            left = gathered[:, columns(c)]
            for start in range(0, width, 256):
                span = pl.ds(start, min(256, width - start))
                part = jnp.dot(left, held[columns(c), span], preferred_element_type=jnp.float32)
                if c == 0:
                    logits[:, span] = part
                else:
                    logits[:, span] += part

    group = 32

    def rows_of(i, carry):
        at = pl.ds(pl.multiple_of(i * group, group), group)
        own_pick = pick[at, :] - me * width
        own_pick = jnp.concatenate([own_pick] * (LANES // picks), axis=1)
        tile, lane = own_pick >> 7, own_pick & (LANES - 1)
        tiles = [logits[at, pl.ds(v * LANES, LANES)] for v in range(width // LANES)]
        top = functools.reduce(jnp.maximum, tiles)
        top = jnp.max(top, axis=1, keepdims=True)
        total = functools.reduce(jnp.add, [jnp.exp(x - top) for x in tiles])
        total = jnp.sum(total, axis=1, keepdims=True)
        found = jnp.zeros((group, LANES), jnp.float32)
        for v, x in enumerate(tiles):
            found = jnp.where(tile == v, jnp.take_along_axis(x, lane, axis=1, mode="promise_in_bounds"), found)
        at_lane = lax.broadcasted_iota(jnp.int32, (group, LANES), 1)
        found = jnp.where(at_lane == picks, top, found)
        found = jnp.where(at_lane == picks + 1, total, found)
        stage[at, :] = found
        return carry

    lax.fori_loop(0, tokens // group, rows_of, 0)

    def permute(i, carry):
        for k in range(8):
            r = i * 8 + k
            outbox[pl.ds(r, 1), :] = stage[pl.ds(order[r], 1), :]
        return carry

    lax.fori_loop(0, tokens // 8, permute, 0)

    end = []
    for j in range(1, n):
        to = lax.rem(me + j, n)
        copy = pltpu.make_async_remote_copy(
            src_ref=outbox.at[pl.ds(pl.multiple_of(to * rows, rows), rows), :], dst_ref=inbox.at[j - 1],
            send_sem=end_send.at[j - 1], recv_sem=end_recv.at[j - 1],
            device_id={"vocab": to}, device_id_type=MESH,
        )
        copy.start()
        end.append(copy)
    for c in range(chunks):
        for copy in far[c] + near[c]:
            copy.wait_send()
    for copy in end:
        copy.wait_recv()
    parts = [outbox[pl.ds(pl.multiple_of(me * rows, rows), rows), :]] + [inbox[j] for j in range(n - 1)]
    tops = [x[:, picks:picks + 1] for x in parts]
    top = functools.reduce(jnp.maximum, tops)
    total = functools.reduce(jnp.add, [x[:, picks + 1:picks + 2] * jnp.exp(t - top) for x, t in zip(parts, tops)])
    log_total = top + jnp.log(total)
    logprobs[...] = functools.reduce(jnp.add, [x[:, :picks] for x in parts]) - log_total
    diagonal = lax.broadcasted_iota(jnp.int32, (rows, rows), 0) == lax.broadcasted_iota(jnp.int32, (rows, rows), 1)
    logtotal[...] = jnp.sum(jnp.where(diagonal, log_total, 0.0), axis=0, keepdims=True)
    for copy in end:
        copy.wait_send()


def local(hidden_states, head_weight, pick_index, owner_order):
    n = lax.axis_size("vocab")
    rows, depth = hidden_states.shape
    width = head_weight.shape[1]
    tokens, picks = pick_index.shape
    chunks = 8
    pair = 2 if n % 2 == 0 else 1
    outer = n // pair
    dma = pltpu.SemaphoreType.DMA
    logprobs, logtotal = pl.pallas_call(
        functools.partial(kernel, n, chunks),
        out_shape=(
            jax.ShapeDtypeStruct((rows, picks), jnp.float32),
            jax.ShapeDtypeStruct((1, rows), jnp.float32),
        ),
        in_specs=[
            pl.BlockSpec(memory_space=pl.ANY),
            pl.BlockSpec(memory_space=pl.ANY),
            pl.BlockSpec(memory_space=pltpu.VMEM),
            pl.BlockSpec(memory_space=pltpu.SMEM),
        ],
        out_specs=(pl.BlockSpec(memory_space=pltpu.VMEM), pl.BlockSpec(memory_space=pltpu.VMEM)),
        scratch_shapes=[
            pltpu.VMEM((tokens, depth), jnp.bfloat16),
            pltpu.VMEM((depth, width), jnp.bfloat16),
            pltpu.VMEM((tokens, width), jnp.float32),
            pltpu.VMEM((tokens, LANES), jnp.float32),
            pltpu.VMEM((tokens, LANES), jnp.float32),
            pltpu.VMEM((n - 1, rows, LANES), jnp.float32),
            dma((chunks,)),
            dma(()),
            dma((chunks, max(outer - 1, 1))),
            dma((chunks, max(outer - 1, 1))),
            dma((chunks, outer)),
            dma((chunks, outer)),
            dma((n - 1,)),
            dma((n - 1,)),
        ],
        compiler_params=pltpu.CompilerParams(
            collective_id=0, has_side_effects=True, vmem_limit_bytes=60 * 1024 * 1024
        ),
    )(hidden_states, head_weight, pick_index, owner_order)
    return logprobs, logtotal.reshape(rows)


def solution(mesh):
    in_specs = (P(("group", "vocab"), None), P(None, "vocab"), P("group", None), P("group"))
    out_specs = (P(("group", "vocab"), None), P(("group", "vocab")))
    return jax.shard_map(local, mesh=mesh, in_specs=in_specs, out_specs=out_specs, check_vma=False)
```

time: 114 us -> 41.3 us (0.36)
  waiting for transfers between devices: 56.6 us -> 0 us
  Pallas kernels: 0 us -> 36.5 us
  other arithmetic: 14.3 us -> 0 us
  between operations: 14.1 us -> 0.64 us
  starting transfers between devices: 12.7 us -> 0 us
  matrix products: 9.97 us -> 0 us
  local copies, waits for them, and re-layouts: 6.11 us -> 3.88 us
    all_gather x1 -> x0, waiting for transfers between devices: 43.7 us -> none  [local(): lax.all_gather(hidden_states, 'vocab', axis=0, tiled=True)]
    pallas_call x0 -> x1, Pallas kernels: none -> 36.5 us  [local(): pl.pallas_call(functools.partial(kernel, n, chunks), out_shape=(jax.Shape...]
    all_to_all x3 -> x0, starting transfers between devices: 12.6 us -> none  [the longest x1 5.98 us: local(): lax.all_to_all(sent_sum, 'vocab', split_axis=0, concat_axis=0, tiled=True)]
    all_to_all x3 -> x0, waiting for transfers between devices: 12.2 us -> none  [the longest x1 6.58 us: local(): lax.all_to_all(sent_picks, 'vocab', split_axis=0, concat_axis=0, tiled=True)]
    reduce_sum x7 -> x0, other arithmetic: 11.4 us -> none  [the longest x4 11 us: select_block(): return jnp.sum(jnp.where(matches, block_logits[:, None, :], 0.0), axis=2)]
    dot_general x1 -> x0, matrix products: 9.97 us -> none  [local(): jnp.dot(lax.all_gather(hidden_states, 'vocab', axis=0, tiled=True), head_...]
    gather x3 -> x0, local copies, waits for them, and re-layouts: 3.1 us -> none  [the longest x1 1.23 us: local(): jnp.take(local_max, owner_order, axis=0).reshape(shard_count, own_rows)]
    unnamed x6 -> x3, local copies, waits for them, and re-layouts: 0.79 us -> 3.88 us
  transfers between devices with their start and end apart: 4 -> 0, of which waited for: 3 -> 0; matrix products, arithmetic and copies ran while one was open for 13% -> 0% of each run, Pallas kernels for 0% -> 0%
where the time goes in v1:
time: 41.3 us; the launch traced here: 41 us
  Pallas kernels  36.5 us (88%)
  local copies, waits for them, and re-layouts  3.88 us (9%)
  between operations  0.64 us (2%)
    pallas_call x1, Pallas kernels, local(): pl.pallas_call(functools.partial(kernel, n, chunks), out_shape=(jax.Shape...  36.5 us
    unnamed x3, local copies, waits for them, and re-layouts  3.88 us

profile of v1, /device:TPU:0, one launch (start us, length us, event | category | flops | bytes accessed | tf_op | source)
XLA Modules:
  0.0 41.0 jit_solution(2560598185150394777)
XLA Ops:
  0.6 1.5 %copy.6.pick = s32[128,64]{1,0:T(8,128)} copy(s32[128,64]{0,1:T(8,128)} %param.6) | data formatting | bytes 65536 | tf_op args[2]
  2.1 36.5 %shard_map.59 = (f32[16,64]{1,0:T(8,128)}, f32[1,16]{1,0:T(1,128)}) custom-call(bf16[16,4096]{1,0:T(8,128)(2,1)} %hid.1, bf16[4096,2432]{1,0:T(8,128)(2,1)} %weight.1, s32[128,64]{1,0:T(8,128)} %copy.6.pick, s32[128]{0:T(128)} %order.1), custom_call_target="tpu_custom_call" | custom-call | tf_op jit(solution)/shard_map/pallas_call | solution.py:168
  38.6 1.3 %copy.9 = f32[16,64]{1,0:T(8,128)} copy(f32[16,64]{1,0:T(8,128)} %get-tuple-element.8) | data formatting | bytes 8192
  39.9 1.1 %copy.10 = f32[16]{0:T(128)} copy(f32[16]{0:T(128)} %bitcast.1) | data formatting | bytes 128

commit v2 on v1

--- a/solution.py
+++ b/solution.py
@@ -15,14 +15,14 @@
     n, chunks,
     hid, weight, pick, order,
     logprobs, logtotal,
-    gathered, held, logits, stage, outbox, inbox,
-    weight_sem, own_sem, far_send, far_recv, near_send, near_recv, end_send, end_recv,
+    gathered, held, logits, wanted, stage, outbox, inbox,
+    weight_sem, own_sem, up_send, up_recv, down_send, down_recv, near_send, near_recv, end_send, end_recv,
 ):
     me = lax.axis_index("vocab")
     rows, depth = hid.shape
     tokens = gathered.shape[0]
     width = weight.shape[1]
-    picks = pick.shape[1]
+    picks = pick.shape[0]
     kc = depth // chunks
     pair = 2 if n % 2 == 0 else 1
     outer = n // pair
@@ -46,64 +46,87 @@
     barrier = pltpu.get_barrier_semaphore()
     for j in range(1, n):
         pl.semaphore_signal(barrier, inc=1, device_id={"vocab": lax.rem(me + j, n)}, device_id_type=MESH)
+    wanted[...] = jnp.concatenate([pick[...]] * (LANES // picks), axis=0).T - me * width
     pl.semaphore_wait(barrier, n - 1)
 
-    far = [[] for _ in range(chunks)]
-    near = [[] for _ in range(chunks)]
-    for c in range(chunks):
-        for j in range(1, outer):
-            copy = pltpu.make_async_remote_copy(
-                src_ref=hid.at[:, columns(c)], dst_ref=block(me, c),
-                send_sem=far_send.at[c, j - 1], recv_sem=far_recv.at[c, j - 1],
-                device_id={"vocab": lax.rem(pos + j, outer) * pair + side}, device_id_type=MESH,
-            )
-            copy.start()
-            far[c].append(copy)
+    def far(sems, c, d, step, hop):
+        owner = (pos - step * d) * pair + side
+        there = block(owner, c)
+        send, recv = sems
+        return pltpu.make_async_remote_copy(
+            src_ref=hid.at[:, columns(c)] if d == 0 else there, dst_ref=there,
+            send_sem=send.at[c, d], recv_sem=recv.at[c, d + hop],
+            device_id={"vocab": lax.rem(me + step * pair + n, n)}, device_id_type=MESH,
+        )
+
+    def near(c, owner, slot):
+        there = block(owner, c)
+        return pltpu.make_async_remote_copy(
+            src_ref=hid.at[:, columns(c)] if slot == 0 else there, dst_ref=there,
+            send_sem=near_send.at[c, slot], recv_sem=near_recv.at[c, slot],
+            device_id={"vocab": partner}, device_id_type=MESH,
+        )
+
+    lines = (
+        ((up_send, up_recv), 1, 0, lambda d: pos >= d, pos < outer - 1),
+        ((down_send, down_recv), -1, outer - 1, lambda d: pos + d < outer, pos > 0),
+    )
+    for c in range(chunks):
+        for sems, step, base, has, onward in lines:
+            if outer > 1:
+                @pl.when(onward)
+                def _():
+                    far(sems, c, 0, step, 0).start()
         if pair == 2:
-            copy = pltpu.make_async_remote_copy(
-                src_ref=hid.at[:, columns(c)], dst_ref=block(me, c),
-                send_sem=near_send.at[c, 0], recv_sem=near_recv.at[c, 0],
-                device_id={"vocab": partner}, device_id_type=MESH,
-            )
-            copy.start()
-            near[c].append(copy)
-
-    for step in range(chunks + 1):
-        if step < chunks:
-            c = step
-            for j in range(1, outer):
-                far[c][j - 1].wait_recv()
+            near(c, me, 0).start()
+
+    def relay(c, d):
+        for sems, step, base, has, onward in lines:
+            @pl.when(has(d))
+            def _():
+                far(sems, c, d, step, -1).wait_recv()
+                if d < outer - 1:
+                    @pl.when(onward)
+                    def _():
+                        far(sems, c, d, step, 0).start()
                 if pair == 2:
-                    source = lax.rem(pos - j + outer, outer) * pair + side
-                    copy = pltpu.make_async_remote_copy(
-                        src_ref=block(source, c), dst_ref=block(source, c),
-                        send_sem=near_send.at[c, j], recv_sem=near_recv.at[c, j],
-                        device_id={"vocab": partner}, device_id_type=MESH,
-                    )
-                    copy.start()
-                    near[c].append(copy)
-        if step >= 1:
-            c = step - 1
+                    near(c, (pos - step * d) * pair + side, base + d).start()
+
+    def multiply(c):
+        if c == 0:
+            own.wait()
+        if pair == 2:
+            near(c, me + 1 - 2 * side, 0).wait_recv()
+            for d in range(1, outer):
+                for sems, step, base, has, onward in lines:
+                    @pl.when(has(d))
+                    def _():
+                        near(c, (pos - step * d) * pair + 1 - side, base + d).wait_recv()
+        weight_copies[c].wait()
+        left = gathered[:, columns(c)]
+        for start in range(0, width, 256):
+            span = pl.ds(start, min(256, width - start))
+            part = jnp.dot(left, held[columns(c), span], preferred_element_type=jnp.float32)
             if c == 0:
-                own.wait()
-            for copy in near[c]:
-                copy.wait_recv()
-            weight_copies[c].wait()
-            left = gathered[:, columns(c)]
-            for start in range(0, width, 256):
-                span = pl.ds(start, min(256, width - start))
-                part = jnp.dot(left, held[columns(c), span], preferred_element_type=jnp.float32)
-                if c == 0:
-                    logits[:, span] = part
-                else:
-                    logits[:, span] += part
+                logits[:, span] = part
+            else:
+                logits[:, span] += part
+
+    for d in range(1, outer - 1):
+        for c in range(chunks):
+            relay(c, d)
+    for c in range(chunks):
+        if outer > 1:
+            relay(c, outer - 1)
+        if c >= 1:
+            multiply(c - 1)
+    multiply(chunks - 1)
 
     group = 32
 
     def rows_of(i, carry):
         at = pl.ds(pl.multiple_of(i * group, group), group)
-        own_pick = pick[at, :] - me * width
-        own_pick = jnp.concatenate([own_pick] * (LANES // picks), axis=1)
+        own_pick = wanted[at, :]
         tile, lane = own_pick >> 7, own_pick & (LANES - 1)
         tiles = [logits[at, pl.ds(v * LANES, LANES)] for v in range(width // LANES)]
         top = functools.reduce(jnp.maximum, tiles)
@@ -140,8 +163,18 @@
         copy.start()
         end.append(copy)
     for c in range(chunks):
-        for copy in far[c] + near[c]:
-            copy.wait_send()
+        if pair == 2:
+            near(c, me, 0).wait_send()
+        for sems, step, base, has, onward in lines:
+            for d in range(outer - 1):
+                @pl.when(jnp.logical_and(has(d), onward))
+                def _():
+                    far(sems, c, d, step, 0).wait_send()
+            if pair == 2:
+                for d in range(1, outer):
+                    @pl.when(has(d))
+                    def _():
+                        near(c, (pos - step * d) * pair + side, base + d).wait_send()
     for copy in end:
         copy.wait_recv()
     parts = [outbox[pl.ds(pl.multiple_of(me * rows, rows), rows), :]] + [inbox[j] for j in range(n - 1)]
@@ -156,12 +189,17 @@
         copy.wait_send()
 
 
+def finish(logprobs, logtotal, logprobs_out, logtotal_out):
+    logprobs_out[...] = logprobs[...]
+    logtotal_out[...] = logtotal[...]
+
+
 def local(hidden_states, head_weight, pick_index, owner_order):
     n = lax.axis_size("vocab")
     rows, depth = hidden_states.shape
     width = head_weight.shape[1]
     tokens, picks = pick_index.shape
-    chunks = 8
+    chunks = 2
     pair = 2 if n % 2 == 0 else 1
     outer = n // pair
     dma = pltpu.SemaphoreType.DMA
@@ -182,22 +220,32 @@
             pltpu.VMEM((tokens, depth), jnp.bfloat16),
             pltpu.VMEM((depth, width), jnp.bfloat16),
             pltpu.VMEM((tokens, width), jnp.float32),
+            pltpu.VMEM((tokens, LANES), jnp.int32),
             pltpu.VMEM((tokens, LANES), jnp.float32),
             pltpu.VMEM((tokens, LANES), jnp.float32),
             pltpu.VMEM((n - 1, rows, LANES), jnp.float32),
             dma((chunks,)),
             dma(()),
-            dma((chunks, max(outer - 1, 1))),
-            dma((chunks, max(outer - 1, 1))),
-            dma((chunks, outer)),
-            dma((chunks, outer)),
+            dma((chunks, outer)),
+            dma((chunks, outer)),
+            dma((chunks, outer)),
+            dma((chunks, outer)),
+            dma((chunks, 2 * outer - 1)),
+            dma((chunks, 2 * outer - 1)),
             dma((n - 1,)),
             dma((n - 1,)),
         ],
         compiler_params=pltpu.CompilerParams(
             collective_id=0, has_side_effects=True, vmem_limit_bytes=60 * 1024 * 1024
         ),
-    )(hidden_states, head_weight, pick_index, owner_order)
+    )(hidden_states, head_weight, pick_index.T, owner_order)
+    logprobs, logtotal = pl.pallas_call(
+        finish,
+        out_shape=(
+            jax.ShapeDtypeStruct((rows, picks), jnp.float32),
+            jax.ShapeDtypeStruct((1, rows), jnp.float32),
+        ),
+    )(logprobs, logtotal)
     return logprobs, logtotal.reshape(rows)
 
 

time: 41.3 us -> 32.7 us (0.79)
  Pallas kernels: 36.5 us -> 31.8 us
  local copies, waits for them, and re-layouts: 3.88 us -> 0 us
    pallas_call x1, Pallas kernels: 36.5 us -> 30.5 us  [local(): pl.pallas_call(functools.partial(kernel, n, chunks), out_shape=(jax.Shape...]
    unnamed x3 -> x0, local copies, waits for them, and re-layouts: 3.88 us -> none
    pallas_call x0 -> x1, Pallas kernels: none -> 1.3 us  [local(): pl.pallas_call(finish, out_shape=(jax.ShapeDtypeStruct((rows, picks), jnp...]
where the time goes in v2:
time: 32.7 us; the launch traced here: 32.4 us
  Pallas kernels  31.8 us (97%)
  between operations  0.64 us (2%)
    pallas_call x1, Pallas kernels, local(): pl.pallas_call(functools.partial(kernel, n, chunks), out_shape=(jax.Shape...  30.5 us
    pallas_call x1, Pallas kernels, local(): pl.pallas_call(finish, out_shape=(jax.ShapeDtypeStruct((rows, picks), jnp...  1.3 us

profile of v2, /device:TPU:0, one launch (start us, length us, event | category | flops | bytes accessed | tf_op | source)
XLA Modules:
  0.0 32.4 jit_solution(16562194476782463040)
XLA Ops:
  0.6 30.5 %shard_map.59 = (f32[16,64]{1,0:T(8,128)}, f32[1,16]{1,0:T(1,128)}) custom-call(bf16[16,4096]{1,0:T(8,128)(2,1)} %hid.1, bf16[4096,2432]{1,0:T(8,128)(2,1)} %weight.1, s32[64,128]{1,0:T(8,128)} %bitcast.2, s32[128]{0:T(128)} %order.1), custom_call_target="tpu_custom_call" | custom-call | tf_op jit(solution)/shard_map/pallas_call | solution.py:206
  31.1 1.3 %shard_map.60 = (f32[16,64]{1,0:T(8,128)}, f32[1,16]{1,0:T(1,128)}) custom-call(f32[16,64]{1,0:T(8,128)} %get-tuple-element.6.logprobs, f32[1,16]{1,0:T(1,128)} %get-tuple-element.7.logtotal), custom_call_target="tpu_custom_call" | custom-call | tf_op jit(solution)/shard_map/pallas_call | solution.py:242
